TPU v7x, 32 devices: a whole 2x2x4 slice. The times are simulated.
32 devices in a mesh: ctx: 8 (over z, y), tp: 4 (over x, core).
Axes of the slice: x: 2, y: 2, z: 4, core: 2. Of those that a mesh axis runs over, the one named last changes fastest.
Arguments:
- queries: bfloat16 [2048, 64, 128], P('ctx', 'tp'), may hold values from -48 to 48
- keys: bfloat16 [2048, 8, 128], P('ctx', 'tp'), may hold values from -3 to 3
- values: bfloat16 [2048, 8, 128], P('ctx', 'tp'), may hold values from -6 to 6
- segment_ids: int32 [2048], P('ctx'), may hold values from 0 to 7, never falling along the last dimension, each value on 1 to 1280 neighbouring positions
Outputs:
- attended: bfloat16 [2048, 8192], P(('ctx', 'tp'))
Inputs may be any that keep to these rules, and one draw needn't show every extreme that they name: `segment_ids`: ids never fall along the tokens; each document holds 1 to 1280 tokens, and one holds exactly 1280.
All inputs are finite; a program needn't handle non-finite values.
Results may differ from a plain program's by a relative error of at most 0.003.
Values may be sent and summed in bfloat16 or wider, within the bound.
A program may use at most 64 MiB of HBM per device.

v0:
```python
import math
import jax
import jax.numpy as jnp
from jax import lax
from jax.sharding import PartitionSpec as P


def passed_along(value, axis, by):
    length = lax.axis_size(axis)
    pairs = [(i, i + by) for i in range(length) if 0 <= i + by < length]
    return lax.ppermute(value, axis, pairs)


def attend_rows(state, grouped, seg_q, pos_q, keys, values, seg_k, pos_k, live):
    scale = 1.0 / math.sqrt(grouped.shape[-1])
    high, total, accum = state
    scores = jnp.einsum("tkgd,pkd->kgtp", grouped, keys, preferred_element_type=jnp.float32) * scale
    allowed = (seg_q[:, None] == seg_k[None, :]) & (pos_k[None, :] <= pos_q[:, None]) & live
    scores = jnp.where(allowed, scores, -1e30)
    newtop = jnp.maximum(high, jnp.max(scores, axis=-1))
    factor = jnp.exp(high - newtop)
    weights = jnp.where(allowed, jnp.exp(scores - newtop[..., None]), 0.0)
    total = total * factor + jnp.sum(weights, axis=-1)
    accum = accum * factor[..., None] + jnp.einsum(
        "kgtp,pkd->kgtd", weights.astype(jnp.bfloat16), values, preferred_element_type=jnp.float32
    )
    return (newtop, total, accum)


def fold_piece(state, grouped, seg_q, pos_q, keys, values, seg_k, start, live):
    length = keys.shape[0]
    first = 0 * length
    pos_rows = start + first + lax.iota(jnp.int32, length)
    return attend_rows(state, grouped, seg_q, pos_q, keys, values, seg_k, pos_rows, live)


def local(queries, keys, values, segment_ids):
    rows, heads, head = queries.shape
    groups = keys.shape[1]
    per_group = heads // groups
    ctx_count = lax.axis_size("ctx")
    here = lax.axis_index("ctx")
    grouped = queries.reshape(rows, groups, per_group, head)
    pos_q = here * rows + lax.iota(jnp.int32, rows)
    initial = (
        jnp.full((groups, per_group, rows), -1e30, jnp.float32),
        jnp.zeros((groups, per_group, rows), jnp.float32),
        jnp.zeros((groups, per_group, rows, head), jnp.float32),
    )
    longest = rows * ctx_count * 5 // 8
    reach = min((longest + rows - 1) // rows, ctx_count - 1)
    state = fold_piece(
        initial, grouped, segment_ids, pos_q, keys, values, segment_ids, here * rows, True
    )

    def step(distance, carry):
        state, block = carry
        block = passed_along((block[0], block[1], block[2]), "ctx", 1)
        owner = here - distance
        state = fold_piece(
            state,
            grouped,
            segment_ids,
            pos_q,
            block[0],
            block[1],
            block[2],
            owner * rows,
            owner >= 0,
        )
        return (state, block)

    state, unused = lax.fori_loop(1, reach + 1, step, (state, (keys, values, segment_ids)))
    high, total, accum = state
    result = (accum / total[..., None]).astype(jnp.bfloat16)
    result = jnp.transpose(result, (2, 0, 1, 3)).reshape(rows, heads * head)
    return lax.all_to_all(result, "tp", split_axis=0, concat_axis=1, tiled=True)


def solution(mesh):
    in_specs = (P("ctx", "tp", None), P("ctx", "tp", None), P("ctx", "tp", None), P("ctx"))
    out_specs = P(("ctx", "tp"), None)
    return jax.shard_map(local, mesh=mesh, in_specs=in_specs, out_specs=out_specs, check_vma=False)
```

profile of v0, /device:TPU:0, one launch (start us, length us, event | category | flops | bytes accessed | tf_op | source)
XLA Modules:
  0.0 117.8 jit_solution(8736475935258747422)
XLA Ops:
  6.4 1.9 %copy-done = f32[2,256,256,8]{2,1,3,0:T(8,128)} copy-done((f32[2,256,256,8]{2,1,3,0:T(8,128)}, f32[2,256,256,8]{2,1,3,0:T(8,128)S(1)}, u32[]{:S(2)}) %copy-start) | copy-done | bytes 4194328
  10.1 3.4 %fusion.30 = f32[2,8,256,128]{3,2,1,0:T(8,128)S(1)} fusion(f32[2,256,256,8]{2,1,3,0:T(8,128)} %copy-done, f32[2,8,256]{2,1,0:T(8,128)S(1)} %broadcast_maximum_fusion, pred[256,256]{0,1:T(8,128)(4,1)S(1)} %compare_and_fusion, f32[2,8,256]{2,1,0:T(8,128)S(1)} %get-tuple-element.278, bf16[256,2,128,1]{2,1,0,3:T(2,128)(2,1)S(1)} %bitcast.66), kind=kOutput, calls=%fused_computation.36 | convolution fusion | flops 274202624 | bytes 6520832 | tf_op jit(solution)/shard_map/kgtp,pkd->kgtd/dot_general | solution.py:24
  13.5 84.3 %while.24 = (s32[]{:T(128)}, f32[2,8,256]{2,1,0:T(8,128)S(1)}, f32[2,8,256]{2,1,0:T(8,128)S(1)}, f32[2,8,256,128]{3,2,1,0:T(8,128)S(1)}, bf16[256,2,128]{2,0,1:T...) while((s32[]{:T(128)}, f32[2,8,256]{2,1,0:T(8,128)S(1)}, ...), condition=%wide.region_5.6_spmd.clone, body=%wide.region_2.5_spmd.clone.sunk | while | flops 551821824 | bytes 20197672 | solution.py:73
  13.5 4.9 %collective-permute-start = (s32[256]{0:T(256)S(1)}, s32[256]{0:T(256)S(1)}, u32[]{:S(2)}, u32[]{:S(2)}) collective-permute-start(s32[256]{0:T(256)S(1)} %get-tuple-element.381), channel_id=1, source_target_pairs={{0,4},{4,8},{8,12},{12,16},{16,20},{20,24},{24,28},{1,5},{5,9},{9,... | collective-permute-start | bytes 3080 | tf_op jit(solution)/shard_map/while/body/eval_jaxpr/ppermute | solution.py:11
  18.4 3.4 %collective-permute-start.1 = (bf16[256,2,128]{2,0,1:T(8,128)(2,1)}, bf16[256,2,128]{2,0,1:T(8,128)(2,1)S(1)}, u32[]{:S(2)}, u32[]{:S(2)}) collective-permute-start(bf16[256,2,128]{2,0,1:T(8,128)(2,1)} %get-tuple-element.379), channel_id=1, source_target_pairs={{0,4},{4,8},{8,12},{12,16},{16,20},{20,24},{24,28},{1,5},{5,9},{9,... | collective-permute-start | bytes 393224 | tf_op jit(solution)/shard_map/while/body/eval_jaxpr/ppermute | solution.py:11
  21.9 3.4 %collective-permute-start.2 = (bf16[256,2,128]{2,0,1:T(8,128)(2,1)}, bf16[256,2,128]{2,0,1:T(8,128)(2,1)S(1)}, u32[]{:S(2)}, u32[]{:S(2)}) collective-permute-start(bf16[256,2,128]{2,0,1:T(8,128)(2,1)} %get-tuple-element.380), channel_id=1, source_target_pairs={{0,4},{4,8},{8,12},{12,16},{16,20},{20,24},{24,28},{1,5},{5,9},{9,... | collective-permute-start | bytes 393224 | tf_op jit(solution)/shard_map/while/body/eval_jaxpr/ppermute | solution.py:11
  28.8 1.9 %multiply_add_fusion.5 = f32[2,8,256,128]{3,2,1,0:T(8,128)S(1)} fusion(f32[2,8,256,128]{3,2,1,0:T(8,128)S(1)} %get-tuple-element.378, f32[2,256,256,8]{2,1,3,0:T(8,128)S(1)} %get-tuple-element.358, f32[2,8,256]{2,1,0:T(8,128)S(1)} %max.9, pred[256,256]{0,1:T(8,128)(4,1)S(1)} %and_and_fusion.2, f32[2,8,256]{2,1,0:T(8,128)S(1)} %get-tuple-element.360, ...), kind=kOutput, calls=%fused_computation.7.clone.1 | convolution fusion | flops 274726912 | bytes 8617984 | tf_op jit(solution)/shard_map/while/body/eval_jaxpr/kgtp,pkd->kgtd/dot_general | solution.py:24
  30.6 4.2 %collective-permute-start = (s32[256]{0:T(256)S(1)}, s32[256]{0:T(256)S(1)}, u32[]{:S(2)}, u32[]{:S(2)}) collective-permute-start(s32[256]{0:T(256)S(1)} %get-tuple-element.381), channel_id=1, source_target_pairs={{0,4},{4,8},{8,12},{12,16},{16,20},{20,24},{24,28},{1,5},{5,9},{9,... | collective-permute-start | bytes 3080 | tf_op jit(solution)/shard_map/while/body/eval_jaxpr/ppermute | solution.py:11
  34.9 4.3 %collective-permute-start.1 = (bf16[256,2,128]{2,0,1:T(8,128)(2,1)}, bf16[256,2,128]{2,0,1:T(8,128)(2,1)S(1)}, u32[]{:S(2)}, u32[]{:S(2)}) collective-permute-start(bf16[256,2,128]{2,0,1:T(8,128)(2,1)} %get-tuple-element.379), channel_id=1, source_target_pairs={{0,4},{4,8},{8,12},{12,16},{16,20},{20,24},{24,28},{1,5},{5,9},{9,... | collective-permute-start | bytes 393224 | tf_op jit(solution)/shard_map/while/body/eval_jaxpr/ppermute | solution.py:11
  39.2 2.5 %collective-permute-start.2 = (bf16[256,2,128]{2,0,1:T(8,128)(2,1)}, bf16[256,2,128]{2,0,1:T(8,128)(2,1)S(1)}, u32[]{:S(2)}, u32[]{:S(2)}) collective-permute-start(bf16[256,2,128]{2,0,1:T(8,128)(2,1)} %get-tuple-element.380), channel_id=1, source_target_pairs={{0,4},{4,8},{8,12},{12,16},{16,20},{20,24},{24,28},{1,5},{5,9},{9,... | collective-permute-start | bytes 393224 | tf_op jit(solution)/shard_map/while/body/eval_jaxpr/ppermute | solution.py:11
  45.7 1.9 %multiply_add_fusion.5 = f32[2,8,256,128]{3,2,1,0:T(8,128)S(1)} fusion(f32[2,8,256,128]{3,2,1,0:T(8,128)S(1)} %get-tuple-element.378, f32[2,256,256,8]{2,1,3,0:T(8,128)S(1)} %get-tuple-element.358, f32[2,8,256]{2,1,0:T(8,128)S(1)} %max.9, pred[256,256]{0,1:T(8,128)(4,1)S(1)} %and_and_fusion.2, f32[2,8,256]{2,1,0:T(8,128)S(1)} %get-tuple-element.360, ...), kind=kOutput, calls=%fused_computation.7.clone.1 | convolution fusion | flops 274726912 | bytes 8617984 | tf_op jit(solution)/shard_map/while/body/eval_jaxpr/kgtp,pkd->kgtd/dot_general | solution.py:24
  47.6 4.3 %collective-permute-start = (s32[256]{0:T(256)S(1)}, s32[256]{0:T(256)S(1)}, u32[]{:S(2)}, u32[]{:S(2)}) collective-permute-start(s32[256]{0:T(256)S(1)} %get-tuple-element.381), channel_id=1, source_target_pairs={{0,4},{4,8},{8,12},{12,16},{16,20},{20,24},{24,28},{1,5},{5,9},{9,... | collective-permute-start | bytes 3080 | tf_op jit(solution)/shard_map/while/body/eval_jaxpr/ppermute | solution.py:11
  51.9 4.7 %collective-permute-start.1 = (bf16[256,2,128]{2,0,1:T(8,128)(2,1)}, bf16[256,2,128]{2,0,1:T(8,128)(2,1)S(1)}, u32[]{:S(2)}, u32[]{:S(2)}) collective-permute-start(bf16[256,2,128]{2,0,1:T(8,128)(2,1)} %get-tuple-element.379), channel_id=1, source_target_pairs={{0,4},{4,8},{8,12},{12,16},{16,20},{20,24},{24,28},{1,5},{5,9},{9,... | collective-permute-start | bytes 393224 | tf_op jit(solution)/shard_map/while/body/eval_jaxpr/ppermute | solution.py:11
  56.6 2.1 %collective-permute-start.2 = (bf16[256,2,128]{2,0,1:T(8,128)(2,1)}, bf16[256,2,128]{2,0,1:T(8,128)(2,1)S(1)}, u32[]{:S(2)}, u32[]{:S(2)}) collective-permute-start(bf16[256,2,128]{2,0,1:T(8,128)(2,1)} %get-tuple-element.380), channel_id=1, source_target_pairs={{0,4},{4,8},{8,12},{12,16},{16,20},{20,24},{24,28},{1,5},{5,9},{9,... | collective-permute-start | bytes 393224 | tf_op jit(solution)/shard_map/while/body/eval_jaxpr/ppermute | solution.py:11
  62.6 1.9 %multiply_add_fusion.5 = f32[2,8,256,128]{3,2,1,0:T(8,128)S(1)} fusion(f32[2,8,256,128]{3,2,1,0:T(8,128)S(1)} %get-tuple-element.378, f32[2,256,256,8]{2,1,3,0:T(8,128)S(1)} %get-tuple-element.358, f32[2,8,256]{2,1,0:T(8,128)S(1)} %max.9, pred[256,256]{0,1:T(8,128)(4,1)S(1)} %and_and_fusion.2, f32[2,8,256]{2,1,0:T(8,128)S(1)} %get-tuple-element.360, ...), kind=kOutput, calls=%fused_computation.7.clone.1 | convolution fusion | flops 274726912 | bytes 8617984 | tf_op jit(solution)/shard_map/while/body/eval_jaxpr/kgtp,pkd->kgtd/dot_general | solution.py:24
  64.5 4.3 %collective-permute-start = (s32[256]{0:T(256)S(1)}, s32[256]{0:T(256)S(1)}, u32[]{:S(2)}, u32[]{:S(2)}) collective-permute-start(s32[256]{0:T(256)S(1)} %get-tuple-element.381), channel_id=1, source_target_pairs={{0,4},{4,8},{8,12},{12,16},{16,20},{20,24},{24,28},{1,5},{5,9},{9,... | collective-permute-start | bytes 3080 | tf_op jit(solution)/shard_map/while/body/eval_jaxpr/ppermute | solution.py:11
  68.8 5.2 %collective-permute-start.1 = (bf16[256,2,128]{2,0,1:T(8,128)(2,1)}, bf16[256,2,128]{2,0,1:T(8,128)(2,1)S(1)}, u32[]{:S(2)}, u32[]{:S(2)}) collective-permute-start(bf16[256,2,128]{2,0,1:T(8,128)(2,1)} %get-tuple-element.379), channel_id=1, source_target_pairs={{0,4},{4,8},{8,12},{12,16},{16,20},{20,24},{24,28},{1,5},{5,9},{9,... | collective-permute-start | bytes 393224 | tf_op jit(solution)/shard_map/while/body/eval_jaxpr/ppermute | solution.py:11
  74.0 1.9 %collective-permute-start.2 = (bf16[256,2,128]{2,0,1:T(8,128)(2,1)}, bf16[256,2,128]{2,0,1:T(8,128)(2,1)S(1)}, u32[]{:S(2)}, u32[]{:S(2)}) collective-permute-start(bf16[256,2,128]{2,0,1:T(8,128)(2,1)} %get-tuple-element.380), channel_id=1, source_target_pairs={{0,4},{4,8},{8,12},{12,16},{16,20},{20,24},{24,28},{1,5},{5,9},{9,... | collective-permute-start | bytes 393224 | tf_op jit(solution)/shard_map/while/body/eval_jaxpr/ppermute | solution.py:11
  79.9 1.9 %multiply_add_fusion.5 = f32[2,8,256,128]{3,2,1,0:T(8,128)S(1)} fusion(f32[2,8,256,128]{3,2,1,0:T(8,128)S(1)} %get-tuple-element.378, f32[2,256,256,8]{2,1,3,0:T(8,128)S(1)} %get-tuple-element.358, f32[2,8,256]{2,1,0:T(8,128)S(1)} %max.9, pred[256,256]{0,1:T(8,128)(4,1)S(1)} %and_and_fusion.2, f32[2,8,256]{2,1,0:T(8,128)S(1)} %get-tuple-element.360, ...), kind=kOutput, calls=%fused_computation.7.clone.1 | convolution fusion | flops 274726912 | bytes 8617984 | tf_op jit(solution)/shard_map/while/body/eval_jaxpr/kgtp,pkd->kgtd/dot_general | solution.py:24
  81.8 4.2 %collective-permute-start = (s32[256]{0:T(256)S(1)}, s32[256]{0:T(256)S(1)}, u32[]{:S(2)}, u32[]{:S(2)}) collective-permute-start(s32[256]{0:T(256)S(1)} %get-tuple-element.381), channel_id=1, source_target_pairs={{0,4},{4,8},{8,12},{12,16},{16,20},{20,24},{24,28},{1,5},{5,9},{9,... | collective-permute-start | bytes 3080 | tf_op jit(solution)/shard_map/while/body/eval_jaxpr/ppermute | solution.py:11
  86.1 3.8 %collective-permute-start.1 = (bf16[256,2,128]{2,0,1:T(8,128)(2,1)}, bf16[256,2,128]{2,0,1:T(8,128)(2,1)S(1)}, u32[]{:S(2)}, u32[]{:S(2)}) collective-permute-start(bf16[256,2,128]{2,0,1:T(8,128)(2,1)} %get-tuple-element.379), channel_id=1, source_target_pairs={{0,4},{4,8},{8,12},{12,16},{16,20},{20,24},{24,28},{1,5},{5,9},{9,... | collective-permute-start | bytes 393224 | tf_op jit(solution)/shard_map/while/body/eval_jaxpr/ppermute | solution.py:11
  89.9 1.9 %collective-permute-start.2 = (bf16[256,2,128]{2,0,1:T(8,128)(2,1)}, bf16[256,2,128]{2,0,1:T(8,128)(2,1)S(1)}, u32[]{:S(2)}, u32[]{:S(2)}) collective-permute-start(bf16[256,2,128]{2,0,1:T(8,128)(2,1)} %get-tuple-element.380), channel_id=1, source_target_pairs={{0,4},{4,8},{8,12},{12,16},{16,20},{20,24},{24,28},{1,5},{5,9},{9,... | collective-permute-start | bytes 393224 | tf_op jit(solution)/shard_map/while/body/eval_jaxpr/ppermute | solution.py:11
  95.9 1.9 %multiply_add_fusion.5 = f32[2,8,256,128]{3,2,1,0:T(8,128)S(1)} fusion(f32[2,8,256,128]{3,2,1,0:T(8,128)S(1)} %get-tuple-element.378, f32[2,256,256,8]{2,1,3,0:T(8,128)S(1)} %get-tuple-element.358, f32[2,8,256]{2,1,0:T(8,128)S(1)} %max.9, pred[256,256]{0,1:T(8,128)(4,1)S(1)} %and_and_fusion.2, f32[2,8,256]{2,1,0:T(8,128)S(1)} %get-tuple-element.360, ...), kind=kOutput, calls=%fused_computation.7.clone.1 | convolution fusion | flops 274726912 | bytes 8617984 | tf_op jit(solution)/shard_map/while/body/eval_jaxpr/kgtp,pkd->kgtd/dot_general | solution.py:24
  99.7 17.0 %all_to_all.19 = bf16[4,64,2048]{2,1,0:T(8,128)(2,1)S(1)} all-to-all(bf16[4,64,2048]{2,1,0:T(8,128)(2,1)S(1)} %all_to_all.14), channel_id=1, replica_groups=mesh['ctx'=8,'tp'=4] {'tp'}, dimensions={0} | all-to-all | bytes 2097152 | tf_op jit(solution)/shard_map/all_to_all | solution.py:77
  (84 shorter events, 30.0 us)
Async XLA Ops:
  4.7 4.7 %copy-start.1 = (bf16[256,2,128]{2,1,0:T(2,128)(2,1)S(1)}, bf16[256,2,128]{2,1,0:T(2,128)(2,1)}, u32[]{:S(2)}) copy-start(bf16[256,2,128]{2,1,0:T(2,128)(2,1)} %param.8) | copy-start | bytes 393220
  6.4 1.9 %copy-start = (f32[2,256,256,8]{2,1,3,0:T(8,128)}, f32[2,256,256,8]{2,1,3,0:T(8,128)S(1)}, u32[]{:S(2)}) copy-start(f32[2,256,256,8]{2,1,3,0:T(8,128)S(1)} %get-tuple-element.281) | copy-start | bytes 12582916
  10.1 3.4 %copy-start.2 = (s32[256]{0:T(256)S(1)}, s32[256]{0:T(256)}, u32[]{:S(2)}) copy-start(s32[256]{0:T(256)} %param.9) | copy-start | bytes 3076
  13.5 11.8 %collective-permute-start = (s32[256]{0:T(256)S(1)}, s32[256]{0:T(256)S(1)}, u32[]{:S(2)}, u32[]{:S(2)}) collective-permute-start(s32[256]{0:T(256)S(1)} %get-tuple-element.381), channel_id=1, source_target_pairs={{0,4},{4,8},{8,12},{12,16},{16,20},{20,24},{24,28},{1,5},{5,9},{9,... | collective-permute-start | bytes 3080 | tf_op jit(solution)/shard_map/while/body/eval_jaxpr/ppermute | solution.py:11
  18.4 7.1 %collective-permute-start.1 = (bf16[256,2,128]{2,0,1:T(8,128)(2,1)}, bf16[256,2,128]{2,0,1:T(8,128)(2,1)S(1)}, u32[]{:S(2)}, u32[]{:S(2)}) collective-permute-start(bf16[256,2,128]{2,0,1:T(8,128)(2,1)} %get-tuple-element.379), channel_id=1, source_target_pairs={{0,4},{4,8},{8,12},{12,16},{16,20},{20,24},{24,28},{1,5},{5,9},{9,... | collective-permute-start | bytes 393224 | tf_op jit(solution)/shard_map/while/body/eval_jaxpr/ppermute | solution.py:11
  21.9 6.2 %collective-permute-start.2 = (bf16[256,2,128]{2,0,1:T(8,128)(2,1)}, bf16[256,2,128]{2,0,1:T(8,128)(2,1)S(1)}, u32[]{:S(2)}, u32[]{:S(2)}) collective-permute-start(bf16[256,2,128]{2,0,1:T(8,128)(2,1)} %get-tuple-element.380), channel_id=1, source_target_pairs={{0,4},{4,8},{8,12},{12,16},{16,20},{20,24},{24,28},{1,5},{5,9},{9,... | collective-permute-start | bytes 393224 | tf_op jit(solution)/shard_map/while/body/eval_jaxpr/ppermute | solution.py:11
  30.6 11.2 %collective-permute-start = (s32[256]{0:T(256)S(1)}, s32[256]{0:T(256)S(1)}, u32[]{:S(2)}, u32[]{:S(2)}) collective-permute-start(s32[256]{0:T(256)S(1)} %get-tuple-element.381), channel_id=1, source_target_pairs={{0,4},{4,8},{8,12},{12,16},{16,20},{20,24},{24,28},{1,5},{5,9},{9,... | collective-permute-start | bytes 3080 | tf_op jit(solution)/shard_map/while/body/eval_jaxpr/ppermute | solution.py:11
  34.9 7.7 %collective-permute-start.1 = (bf16[256,2,128]{2,0,1:T(8,128)(2,1)}, bf16[256,2,128]{2,0,1:T(8,128)(2,1)S(1)}, u32[]{:S(2)}, u32[]{:S(2)}) collective-permute-start(bf16[256,2,128]{2,0,1:T(8,128)(2,1)} %get-tuple-element.379), channel_id=1, source_target_pairs={{0,4},{4,8},{8,12},{12,16},{16,20},{20,24},{24,28},{1,5},{5,9},{9,... | collective-permute-start | bytes 393224 | tf_op jit(solution)/shard_map/while/body/eval_jaxpr/ppermute | solution.py:11
  39.2 5.8 %collective-permute-start.2 = (bf16[256,2,128]{2,0,1:T(8,128)(2,1)}, bf16[256,2,128]{2,0,1:T(8,128)(2,1)S(1)}, u32[]{:S(2)}, u32[]{:S(2)}) collective-permute-start(bf16[256,2,128]{2,0,1:T(8,128)(2,1)} %get-tuple-element.380), channel_id=1, source_target_pairs={{0,4},{4,8},{8,12},{12,16},{16,20},{20,24},{24,28},{1,5},{5,9},{9,... | collective-permute-start | bytes 393224 | tf_op jit(solution)/shard_map/while/body/eval_jaxpr/ppermute | solution.py:11
  47.6 11.2 %collective-permute-start = (s32[256]{0:T(256)S(1)}, s32[256]{0:T(256)S(1)}, u32[]{:S(2)}, u32[]{:S(2)}) collective-permute-start(s32[256]{0:T(256)S(1)} %get-tuple-element.381), channel_id=1, source_target_pairs={{0,4},{4,8},{8,12},{12,16},{16,20},{20,24},{24,28},{1,5},{5,9},{9,... | collective-permute-start | bytes 3080 | tf_op jit(solution)/shard_map/while/body/eval_jaxpr/ppermute | solution.py:11
  51.9 7.6 %collective-permute-start.1 = (bf16[256,2,128]{2,0,1:T(8,128)(2,1)}, bf16[256,2,128]{2,0,1:T(8,128)(2,1)S(1)}, u32[]{:S(2)}, u32[]{:S(2)}) collective-permute-start(bf16[256,2,128]{2,0,1:T(8,128)(2,1)} %get-tuple-element.379), channel_id=1, source_target_pairs={{0,4},{4,8},{8,12},{12,16},{16,20},{20,24},{24,28},{1,5},{5,9},{9,... | collective-permute-start | bytes 393224 | tf_op jit(solution)/shard_map/while/body/eval_jaxpr/ppermute | solution.py:11
  56.6 5.3 %collective-permute-start.2 = (bf16[256,2,128]{2,0,1:T(8,128)(2,1)}, bf16[256,2,128]{2,0,1:T(8,128)(2,1)S(1)}, u32[]{:S(2)}, u32[]{:S(2)}) collective-permute-start(bf16[256,2,128]{2,0,1:T(8,128)(2,1)} %get-tuple-element.380), channel_id=1, source_target_pairs={{0,4},{4,8},{8,12},{12,16},{16,20},{20,24},{24,28},{1,5},{5,9},{9,... | collective-permute-start | bytes 393224 | tf_op jit(solution)/shard_map/while/body/eval_jaxpr/ppermute | solution.py:11
  64.5 11.4 %collective-permute-start = (s32[256]{0:T(256)S(1)}, s32[256]{0:T(256)S(1)}, u32[]{:S(2)}, u32[]{:S(2)}) collective-permute-start(s32[256]{0:T(256)S(1)} %get-tuple-element.381), channel_id=1, source_target_pairs={{0,4},{4,8},{8,12},{12,16},{16,20},{20,24},{24,28},{1,5},{5,9},{9,... | collective-permute-start | bytes 3080 | tf_op jit(solution)/shard_map/while/body/eval_jaxpr/ppermute | solution.py:11
  68.8 8.0 %collective-permute-start.1 = (bf16[256,2,128]{2,0,1:T(8,128)(2,1)}, bf16[256,2,128]{2,0,1:T(8,128)(2,1)S(1)}, u32[]{:S(2)}, u32[]{:S(2)}) collective-permute-start(bf16[256,2,128]{2,0,1:T(8,128)(2,1)} %get-tuple-element.379), channel_id=1, source_target_pairs={{0,4},{4,8},{8,12},{12,16},{16,20},{20,24},{24,28},{1,5},{5,9},{9,... | collective-permute-start | bytes 393224 | tf_op jit(solution)/shard_map/while/body/eval_jaxpr/ppermute | solution.py:11
  74.0 5.3 %collective-permute-start.2 = (bf16[256,2,128]{2,0,1:T(8,128)(2,1)}, bf16[256,2,128]{2,0,1:T(8,128)(2,1)S(1)}, u32[]{:S(2)}, u32[]{:S(2)}) collective-permute-start(bf16[256,2,128]{2,0,1:T(8,128)(2,1)} %get-tuple-element.380), channel_id=1, source_target_pairs={{0,4},{4,8},{8,12},{12,16},{16,20},{20,24},{24,28},{1,5},{5,9},{9,... | collective-permute-start | bytes 393224 | tf_op jit(solution)/shard_map/while/body/eval_jaxpr/ppermute | solution.py:11
  81.8 10.0 %collective-permute-start = (s32[256]{0:T(256)S(1)}, s32[256]{0:T(256)S(1)}, u32[]{:S(2)}, u32[]{:S(2)}) collective-permute-start(s32[256]{0:T(256)S(1)} %get-tuple-element.381), channel_id=1, source_target_pairs={{0,4},{4,8},{8,12},{12,16},{16,20},{20,24},{24,28},{1,5},{5,9},{9,... | collective-permute-start | bytes 3080 | tf_op jit(solution)/shard_map/while/body/eval_jaxpr/ppermute | solution.py:11
  86.1 6.6 %collective-permute-start.1 = (bf16[256,2,128]{2,0,1:T(8,128)(2,1)}, bf16[256,2,128]{2,0,1:T(8,128)(2,1)S(1)}, u32[]{:S(2)}, u32[]{:S(2)}) collective-permute-start(bf16[256,2,128]{2,0,1:T(8,128)(2,1)} %get-tuple-element.379), channel_id=1, source_target_pairs={{0,4},{4,8},{8,12},{12,16},{16,20},{20,24},{24,28},{1,5},{5,9},{9,... | collective-permute-start | bytes 393224 | tf_op jit(solution)/shard_map/while/body/eval_jaxpr/ppermute | solution.py:11
  89.9 5.3 %collective-permute-start.2 = (bf16[256,2,128]{2,0,1:T(8,128)(2,1)}, bf16[256,2,128]{2,0,1:T(8,128)(2,1)S(1)}, u32[]{:S(2)}, u32[]{:S(2)}) collective-permute-start(bf16[256,2,128]{2,0,1:T(8,128)(2,1)} %get-tuple-element.380), channel_id=1, source_target_pairs={{0,4},{4,8},{8,12},{12,16},{16,20},{20,24},{24,28},{1,5},{5,9},{9,... | collective-permute-start | bytes 393224 | tf_op jit(solution)/shard_map/while/body/eval_jaxpr/ppermute | solution.py:11
where the time goes:
time: 118 us
  starting transfers between devices  55.4 us (47%)
  matrix products  18.3 us (16%)
  blocking collectives  17 us (14%)
  local copies, waits for them, and re-layouts  15.2 us (13%)
  other arithmetic  8.57 us (7%)
  waiting for transfers between devices  2.57 us (2%)
    ppermute x15, starting transfers between devices, passed_along(): return lax.ppermute(value, axis, pairs)  55.4 us
    all_to_all x1, blocking collectives, local(): return lax.all_to_all(result, 'tp', split_axis=0, concat_axis=1, tiled=True)  17 us
    dot_general x6, matrix products, attend_rows(): jnp.einsum('kgtp,pkd->kgtd', weights.astype(jnp.bfloat16), values, prefer...  12.8 us
    while x20, local copies, waits for them, and re-layouts  6.59 us
    unnamed x10, local copies, waits for them, and re-layouts  6.36 us
    reduce_sum x6, other arithmetic, attend_rows(): total = total * factor + jnp.sum(weights, axis=-1)  6.12 us
    dot_general x6, matrix products, attend_rows(): jnp.einsum('tkgd,pkd->kgtp', grouped, keys, preferred_element_type=jnp.fl...  5.53 us
    ppermute x15, waiting for transfers between devices, passed_along(): return lax.ppermute(value, axis, pairs)  2.57 us
  transfers between devices with their start and end apart: 15, of which 5 were waited for; matrix products, arithmetic and copies ran while one was open for 11% of the time, Pallas kernels for 0%

commit v1 on v0

--- a/solution.py
+++ b/solution.py
@@ -3,6 +3,13 @@
 import jax.numpy as jnp
 from jax import lax
 from jax.sharding import PartitionSpec as P
+
+
+def stacked_exchange(x, axis, split, join):
+    size = lax.axis_size(axis)
+    blocks = jnp.stack(jnp.split(x, size, axis=split), axis=0)
+    blocks = lax.all_to_all(blocks, axis, split_axis=0, concat_axis=0)
+    return jnp.concatenate(blocks, axis=join)
 
 
 def passed_along(value, axis, by):
@@ -74,7 +81,7 @@
     high, total, accum = state
     result = (accum / total[..., None]).astype(jnp.bfloat16)
     result = jnp.transpose(result, (2, 0, 1, 3)).reshape(rows, heads * head)
-    return lax.all_to_all(result, "tp", split_axis=0, concat_axis=1, tiled=True)
+    return stacked_exchange(result, "tp", 0, 1)
 
 
 def solution(mesh):

time: 118 us -> 119 us (level)
    all_to_all x2 -> x0, local copies, waits for them, and re-layouts: 1.57 us -> none  [local(): return lax.all_to_all(result, 'tp', split_axis=0, concat_axis=1, tiled=True)]
where the time goes in v1:
time: 119 us; the launch traced here: 118 us
  starting transfers between devices  55.4 us (47%)
  matrix products  18.3 us (15%)
  blocking collectives  17 us (14%)
  local copies, waits for them, and re-layouts  15.1 us (13%)
  other arithmetic  8.71 us (7%)
  waiting for transfers between devices  2.57 us (2%)
    ppermute x15, starting transfers between devices, passed_along(): return lax.ppermute(value, axis, pairs)  55.4 us
    all_to_all x1, blocking collectives, stacked_exchange(): blocks = lax.all_to_all(blocks, axis, split_axis=0, concat_axis=0)  17 us
    dot_general x6, matrix products, attend_rows(): jnp.einsum('kgtp,pkd->kgtd', weights.astype(jnp.bfloat16), values, prefer...  12.8 us
    while x20, local copies, waits for them, and re-layouts  6.52 us
    unnamed x10, local copies, waits for them, and re-layouts  6.34 us
    reduce_sum x6, other arithmetic, attend_rows(): total = total * factor + jnp.sum(weights, axis=-1)  6.12 us
    dot_general x6, matrix products, attend_rows(): jnp.einsum('tkgd,pkd->kgtp', grouped, keys, preferred_element_type=jnp.fl...  5.53 us
    ppermute x15, waiting for transfers between devices, passed_along(): return lax.ppermute(value, axis, pairs)  2.57 us
  transfers between devices with their start and end apart: 15, of which 5 were waited for; matrix products, arithmetic and copies ran while one was open for 11% of the time, Pallas kernels for 0%

profile of v1, /device:TPU:0, one launch (start us, length us, event | category | flops | bytes accessed | tf_op | source)
XLA Modules:
  0.0 117.9 jit_solution(1158239947586649523)
XLA Ops:
  6.4 1.9 %copy-done = f32[2,256,256,8]{2,1,3,0:T(8,128)} copy-done((f32[2,256,256,8]{2,1,3,0:T(8,128)}, f32[2,256,256,8]{2,1,3,0:T(8,128)S(1)}, u32[]{:S(2)}) %copy-start) | copy-done | bytes 4194328
  10.0 3.4 %fusion.30 = f32[2,8,256,128]{3,2,1,0:T(8,128)S(1)} fusion(f32[2,256,256,8]{2,1,3,0:T(8,128)} %copy-done, f32[2,8,256]{2,1,0:T(8,128)S(1)} %broadcast_maximum_fusion, pred[256,256]{0,1:T(8,128)(4,1)S(1)} %compare_and_fusion, f32[2,8,256]{2,1,0:T(8,128)S(1)} %get-tuple-element.282, bf16[256,2,128,1]{2,1,0,3:T(2,128)(2,1)S(1)} %bitcast.72), kind=kOutput, calls=%fused_computation.36 | convolution fusion | flops 274202624 | bytes 6520832 | tf_op jit(solution)/shard_map/kgtp,pkd->kgtd/dot_general | solution.py:31
  13.5 84.2 %while.24 = (s32[]{:T(128)}, f32[2,8,256]{2,1,0:T(8,128)S(1)}, f32[2,8,256]{2,1,0:T(8,128)S(1)}, f32[2,8,256,128]{3,2,1,0:T(8,128)S(1)}, bf16[256,2,128]{2,0,1:T...) while((s32[]{:T(128)}, f32[2,8,256]{2,1,0:T(8,128)S(1)}, ...), condition=%wide.region_5.6_spmd.clone, body=%wide.region_2.5_spmd.clone.sunk | while | flops 551821824 | bytes 20197672 | solution.py:80
  13.5 4.9 %collective-permute-start = (s32[256]{0:T(256)S(1)}, s32[256]{0:T(256)S(1)}, u32[]{:S(2)}, u32[]{:S(2)}) collective-permute-start(s32[256]{0:T(256)S(1)} %get-tuple-element.385), channel_id=1, source_target_pairs={{0,4},{4,8},{8,12},{12,16},{16,20},{20,24},{24,28},{1,5},{5,9},{9,... | collective-permute-start | bytes 3080 | tf_op jit(solution)/shard_map/while/body/eval_jaxpr/ppermute | solution.py:18
  18.4 3.4 %collective-permute-start.1 = (bf16[256,2,128]{2,0,1:T(8,128)(2,1)}, bf16[256,2,128]{2,0,1:T(8,128)(2,1)S(1)}, u32[]{:S(2)}, u32[]{:S(2)}) collective-permute-start(bf16[256,2,128]{2,0,1:T(8,128)(2,1)} %get-tuple-element.383), channel_id=1, source_target_pairs={{0,4},{4,8},{8,12},{12,16},{16,20},{20,24},{24,28},{1,5},{5,9},{9,... | collective-permute-start | bytes 393224 | tf_op jit(solution)/shard_map/while/body/eval_jaxpr/ppermute | solution.py:18
  21.8 3.4 %collective-permute-start.2 = (bf16[256,2,128]{2,0,1:T(8,128)(2,1)}, bf16[256,2,128]{2,0,1:T(8,128)(2,1)S(1)}, u32[]{:S(2)}, u32[]{:S(2)}) collective-permute-start(bf16[256,2,128]{2,0,1:T(8,128)(2,1)} %get-tuple-element.384), channel_id=1, source_target_pairs={{0,4},{4,8},{8,12},{12,16},{16,20},{20,24},{24,28},{1,5},{5,9},{9,... | collective-permute-start | bytes 393224 | tf_op jit(solution)/shard_map/while/body/eval_jaxpr/ppermute | solution.py:18
  28.7 1.9 %multiply_add_fusion.5 = f32[2,8,256,128]{3,2,1,0:T(8,128)S(1)} fusion(f32[2,8,256,128]{3,2,1,0:T(8,128)S(1)} %get-tuple-element.382, f32[2,256,256,8]{2,1,3,0:T(8,128)S(1)} %get-tuple-element.362, f32[2,8,256]{2,1,0:T(8,128)S(1)} %max.9, pred[256,256]{0,1:T(8,128)(4,1)S(1)} %and_and_fusion.2, f32[2,8,256]{2,1,0:T(8,128)S(1)} %get-tuple-element.364, ...), kind=kOutput, calls=%fused_computation.7.clone.1 | convolution fusion | flops 274726912 | bytes 8617984 | tf_op jit(solution)/shard_map/while/body/eval_jaxpr/kgtp,pkd->kgtd/dot_general | solution.py:31
  30.6 4.2 %collective-permute-start = (s32[256]{0:T(256)S(1)}, s32[256]{0:T(256)S(1)}, u32[]{:S(2)}, u32[]{:S(2)}) collective-permute-start(s32[256]{0:T(256)S(1)} %get-tuple-element.385), channel_id=1, source_target_pairs={{0,4},{4,8},{8,12},{12,16},{16,20},{20,24},{24,28},{1,5},{5,9},{9,... | collective-permute-start | bytes 3080 | tf_op jit(solution)/shard_map/while/body/eval_jaxpr/ppermute | solution.py:18
  34.9 4.3 %collective-permute-start.1 = (bf16[256,2,128]{2,0,1:T(8,128)(2,1)}, bf16[256,2,128]{2,0,1:T(8,128)(2,1)S(1)}, u32[]{:S(2)}, u32[]{:S(2)}) collective-permute-start(bf16[256,2,128]{2,0,1:T(8,128)(2,1)} %get-tuple-element.383), channel_id=1, source_target_pairs={{0,4},{4,8},{8,12},{12,16},{16,20},{20,24},{24,28},{1,5},{5,9},{9,... | collective-permute-start | bytes 393224 | tf_op jit(solution)/shard_map/while/body/eval_jaxpr/ppermute | solution.py:18
  39.2 2.5 %collective-permute-start.2 = (bf16[256,2,128]{2,0,1:T(8,128)(2,1)}, bf16[256,2,128]{2,0,1:T(8,128)(2,1)S(1)}, u32[]{:S(2)}, u32[]{:S(2)}) collective-permute-start(bf16[256,2,128]{2,0,1:T(8,128)(2,1)} %get-tuple-element.384), channel_id=1, source_target_pairs={{0,4},{4,8},{8,12},{12,16},{16,20},{20,24},{24,28},{1,5},{5,9},{9,... | collective-permute-start | bytes 393224 | tf_op jit(solution)/shard_map/while/body/eval_jaxpr/ppermute | solution.py:18
  45.7 1.9 %multiply_add_fusion.5 = f32[2,8,256,128]{3,2,1,0:T(8,128)S(1)} fusion(f32[2,8,256,128]{3,2,1,0:T(8,128)S(1)} %get-tuple-element.382, f32[2,256,256,8]{2,1,3,0:T(8,128)S(1)} %get-tuple-element.362, f32[2,8,256]{2,1,0:T(8,128)S(1)} %max.9, pred[256,256]{0,1:T(8,128)(4,1)S(1)} %and_and_fusion.2, f32[2,8,256]{2,1,0:T(8,128)S(1)} %get-tuple-element.364, ...), kind=kOutput, calls=%fused_computation.7.clone.1 | convolution fusion | flops 274726912 | bytes 8617984 | tf_op jit(solution)/shard_map/while/body/eval_jaxpr/kgtp,pkd->kgtd/dot_general | solution.py:31
  47.6 4.3 %collective-permute-start = (s32[256]{0:T(256)S(1)}, s32[256]{0:T(256)S(1)}, u32[]{:S(2)}, u32[]{:S(2)}) collective-permute-start(s32[256]{0:T(256)S(1)} %get-tuple-element.385), channel_id=1, source_target_pairs={{0,4},{4,8},{8,12},{12,16},{16,20},{20,24},{24,28},{1,5},{5,9},{9,... | collective-permute-start | bytes 3080 | tf_op jit(solution)/shard_map/while/body/eval_jaxpr/ppermute | solution.py:18
  51.8 4.7 %collective-permute-start.1 = (bf16[256,2,128]{2,0,1:T(8,128)(2,1)}, bf16[256,2,128]{2,0,1:T(8,128)(2,1)S(1)}, u32[]{:S(2)}, u32[]{:S(2)}) collective-permute-start(bf16[256,2,128]{2,0,1:T(8,128)(2,1)} %get-tuple-element.383), channel_id=1, source_target_pairs={{0,4},{4,8},{8,12},{12,16},{16,20},{20,24},{24,28},{1,5},{5,9},{9,... | collective-permute-start | bytes 393224 | tf_op jit(solution)/shard_map/while/body/eval_jaxpr/ppermute | solution.py:18
  56.6 2.1 %collective-permute-start.2 = (bf16[256,2,128]{2,0,1:T(8,128)(2,1)}, bf16[256,2,128]{2,0,1:T(8,128)(2,1)S(1)}, u32[]{:S(2)}, u32[]{:S(2)}) collective-permute-start(bf16[256,2,128]{2,0,1:T(8,128)(2,1)} %get-tuple-element.384), channel_id=1, source_target_pairs={{0,4},{4,8},{8,12},{12,16},{16,20},{20,24},{24,28},{1,5},{5,9},{9,... | collective-permute-start | bytes 393224 | tf_op jit(solution)/shard_map/while/body/eval_jaxpr/ppermute | solution.py:18
  62.5 1.9 %multiply_add_fusion.5 = f32[2,8,256,128]{3,2,1,0:T(8,128)S(1)} fusion(f32[2,8,256,128]{3,2,1,0:T(8,128)S(1)} %get-tuple-element.382, f32[2,256,256,8]{2,1,3,0:T(8,128)S(1)} %get-tuple-element.362, f32[2,8,256]{2,1,0:T(8,128)S(1)} %max.9, pred[256,256]{0,1:T(8,128)(4,1)S(1)} %and_and_fusion.2, f32[2,8,256]{2,1,0:T(8,128)S(1)} %get-tuple-element.364, ...), kind=kOutput, calls=%fused_computation.7.clone.1 | convolution fusion | flops 274726912 | bytes 8617984 | tf_op jit(solution)/shard_map/while/body/eval_jaxpr/kgtp,pkd->kgtd/dot_general | solution.py:31
  64.4 4.3 %collective-permute-start = (s32[256]{0:T(256)S(1)}, s32[256]{0:T(256)S(1)}, u32[]{:S(2)}, u32[]{:S(2)}) collective-permute-start(s32[256]{0:T(256)S(1)} %get-tuple-element.385), channel_id=1, source_target_pairs={{0,4},{4,8},{8,12},{12,16},{16,20},{20,24},{24,28},{1,5},{5,9},{9,... | collective-permute-start | bytes 3080 | tf_op jit(solution)/shard_map/while/body/eval_jaxpr/ppermute | solution.py:18
  68.7 5.2 %collective-permute-start.1 = (bf16[256,2,128]{2,0,1:T(8,128)(2,1)}, bf16[256,2,128]{2,0,1:T(8,128)(2,1)S(1)}, u32[]{:S(2)}, u32[]{:S(2)}) collective-permute-start(bf16[256,2,128]{2,0,1:T(8,128)(2,1)} %get-tuple-element.383), channel_id=1, source_target_pairs={{0,4},{4,8},{8,12},{12,16},{16,20},{20,24},{24,28},{1,5},{5,9},{9,... | collective-permute-start | bytes 393224 | tf_op jit(solution)/shard_map/while/body/eval_jaxpr/ppermute | solution.py:18
  73.9 1.9 %collective-permute-start.2 = (bf16[256,2,128]{2,0,1:T(8,128)(2,1)}, bf16[256,2,128]{2,0,1:T(8,128)(2,1)S(1)}, u32[]{:S(2)}, u32[]{:S(2)}) collective-permute-start(bf16[256,2,128]{2,0,1:T(8,128)(2,1)} %get-tuple-element.384), channel_id=1, source_target_pairs={{0,4},{4,8},{8,12},{12,16},{16,20},{20,24},{24,28},{1,5},{5,9},{9,... | collective-permute-start | bytes 393224 | tf_op jit(solution)/shard_map/while/body/eval_jaxpr/ppermute | solution.py:18
  79.9 1.9 %multiply_add_fusion.5 = f32[2,8,256,128]{3,2,1,0:T(8,128)S(1)} fusion(f32[2,8,256,128]{3,2,1,0:T(8,128)S(1)} %get-tuple-element.382, f32[2,256,256,8]{2,1,3,0:T(8,128)S(1)} %get-tuple-element.362, f32[2,8,256]{2,1,0:T(8,128)S(1)} %max.9, pred[256,256]{0,1:T(8,128)(4,1)S(1)} %and_and_fusion.2, f32[2,8,256]{2,1,0:T(8,128)S(1)} %get-tuple-element.364, ...), kind=kOutput, calls=%fused_computation.7.clone.1 | convolution fusion | flops 274726912 | bytes 8617984 | tf_op jit(solution)/shard_map/while/body/eval_jaxpr/kgtp,pkd->kgtd/dot_general | solution.py:31
  81.8 4.2 %collective-permute-start = (s32[256]{0:T(256)S(1)}, s32[256]{0:T(256)S(1)}, u32[]{:S(2)}, u32[]{:S(2)}) collective-permute-start(s32[256]{0:T(256)S(1)} %get-tuple-element.385), channel_id=1, source_target_pairs={{0,4},{4,8},{8,12},{12,16},{16,20},{20,24},{24,28},{1,5},{5,9},{9,... | collective-permute-start | bytes 3080 | tf_op jit(solution)/shard_map/while/body/eval_jaxpr/ppermute | solution.py:18
  86.0 3.8 %collective-permute-start.1 = (bf16[256,2,128]{2,0,1:T(8,128)(2,1)}, bf16[256,2,128]{2,0,1:T(8,128)(2,1)S(1)}, u32[]{:S(2)}, u32[]{:S(2)}) collective-permute-start(bf16[256,2,128]{2,0,1:T(8,128)(2,1)} %get-tuple-element.383), channel_id=1, source_target_pairs={{0,4},{4,8},{8,12},{12,16},{16,20},{20,24},{24,28},{1,5},{5,9},{9,... | collective-permute-start | bytes 393224 | tf_op jit(solution)/shard_map/while/body/eval_jaxpr/ppermute | solution.py:18
  89.8 1.9 %collective-permute-start.2 = (bf16[256,2,128]{2,0,1:T(8,128)(2,1)}, bf16[256,2,128]{2,0,1:T(8,128)(2,1)S(1)}, u32[]{:S(2)}, u32[]{:S(2)}) collective-permute-start(bf16[256,2,128]{2,0,1:T(8,128)(2,1)} %get-tuple-element.384), channel_id=1, source_target_pairs={{0,4},{4,8},{8,12},{12,16},{16,20},{20,24},{24,28},{1,5},{5,9},{9,... | collective-permute-start | bytes 393224 | tf_op jit(solution)/shard_map/while/body/eval_jaxpr/ppermute | solution.py:18
  95.8 1.9 %multiply_add_fusion.5 = f32[2,8,256,128]{3,2,1,0:T(8,128)S(1)} fusion(f32[2,8,256,128]{3,2,1,0:T(8,128)S(1)} %get-tuple-element.382, f32[2,256,256,8]{2,1,3,0:T(8,128)S(1)} %get-tuple-element.362, f32[2,8,256]{2,1,0:T(8,128)S(1)} %max.9, pred[256,256]{0,1:T(8,128)(4,1)S(1)} %and_and_fusion.2, f32[2,8,256]{2,1,0:T(8,128)S(1)} %get-tuple-element.364, ...), kind=kOutput, calls=%fused_computation.7.clone.1 | convolution fusion | flops 274726912 | bytes 8617984 | tf_op jit(solution)/shard_map/while/body/eval_jaxpr/kgtp,pkd->kgtd/dot_general | solution.py:31
  99.9 17.0 %all_to_all.5 = bf16[4,64,2048]{2,1,0:T(8,128)(2,1)S(1)} all-to-all(bf16[4,64,2048]{2,1,0:T(8,128)(2,1)S(1)} %pad_maximum_fusion), channel_id=1, replica_groups=mesh['ctx'=8,'tp'=4] {'tp'}, dimensions={0} | all-to-all | bytes 2097152 | tf_op jit(solution)/shard_map/all_to_all | solution.py:11
  (92 shorter events, 30.0 us)
Async XLA Ops:
  4.7 4.7 %copy-start.1 = (bf16[256,2,128]{2,1,0:T(2,128)(2,1)S(1)}, bf16[256,2,128]{2,1,0:T(2,128)(2,1)}, u32[]{:S(2)}) copy-start(bf16[256,2,128]{2,1,0:T(2,128)(2,1)} %param.8) | copy-start | bytes 393220
  6.4 1.9 %copy-start = (f32[2,256,256,8]{2,1,3,0:T(8,128)}, f32[2,256,256,8]{2,1,3,0:T(8,128)S(1)}, u32[]{:S(2)}) copy-start(f32[2,256,256,8]{2,1,3,0:T(8,128)S(1)} %get-tuple-element.285) | copy-start | bytes 12582916
  10.0 3.4 %copy-start.2 = (s32[256]{0:T(256)S(1)}, s32[256]{0:T(256)}, u32[]{:S(2)}) copy-start(s32[256]{0:T(256)} %param.9) | copy-start | bytes 3076
  13.5 11.8 %collective-permute-start = (s32[256]{0:T(256)S(1)}, s32[256]{0:T(256)S(1)}, u32[]{:S(2)}, u32[]{:S(2)}) collective-permute-start(s32[256]{0:T(256)S(1)} %get-tuple-element.385), channel_id=1, source_target_pairs={{0,4},{4,8},{8,12},{12,16},{16,20},{20,24},{24,28},{1,5},{5,9},{9,... | collective-permute-start | bytes 3080 | tf_op jit(solution)/shard_map/while/body/eval_jaxpr/ppermute | solution.py:18
  18.4 7.1 %collective-permute-start.1 = (bf16[256,2,128]{2,0,1:T(8,128)(2,1)}, bf16[256,2,128]{2,0,1:T(8,128)(2,1)S(1)}, u32[]{:S(2)}, u32[]{:S(2)}) collective-permute-start(bf16[256,2,128]{2,0,1:T(8,128)(2,1)} %get-tuple-element.383), channel_id=1, source_target_pairs={{0,4},{4,8},{8,12},{12,16},{16,20},{20,24},{24,28},{1,5},{5,9},{9,... | collective-permute-start | bytes 393224 | tf_op jit(solution)/shard_map/while/body/eval_jaxpr/ppermute | solution.py:18
  21.8 6.2 %collective-permute-start.2 = (bf16[256,2,128]{2,0,1:T(8,128)(2,1)}, bf16[256,2,128]{2,0,1:T(8,128)(2,1)S(1)}, u32[]{:S(2)}, u32[]{:S(2)}) collective-permute-start(bf16[256,2,128]{2,0,1:T(8,128)(2,1)} %get-tuple-element.384), channel_id=1, source_target_pairs={{0,4},{4,8},{8,12},{12,16},{16,20},{20,24},{24,28},{1,5},{5,9},{9,... | collective-permute-start | bytes 393224 | tf_op jit(solution)/shard_map/while/body/eval_jaxpr/ppermute | solution.py:18
  30.6 11.2 %collective-permute-start = (s32[256]{0:T(256)S(1)}, s32[256]{0:T(256)S(1)}, u32[]{:S(2)}, u32[]{:S(2)}) collective-permute-start(s32[256]{0:T(256)S(1)} %get-tuple-element.385), channel_id=1, source_target_pairs={{0,4},{4,8},{8,12},{12,16},{16,20},{20,24},{24,28},{1,5},{5,9},{9,... | collective-permute-start | bytes 3080 | tf_op jit(solution)/shard_map/while/body/eval_jaxpr/ppermute | solution.py:18
  34.9 7.7 %collective-permute-start.1 = (bf16[256,2,128]{2,0,1:T(8,128)(2,1)}, bf16[256,2,128]{2,0,1:T(8,128)(2,1)S(1)}, u32[]{:S(2)}, u32[]{:S(2)}) collective-permute-start(bf16[256,2,128]{2,0,1:T(8,128)(2,1)} %get-tuple-element.383), channel_id=1, source_target_pairs={{0,4},{4,8},{8,12},{12,16},{16,20},{20,24},{24,28},{1,5},{5,9},{9,... | collective-permute-start | bytes 393224 | tf_op jit(solution)/shard_map/while/body/eval_jaxpr/ppermute | solution.py:18
  39.2 5.8 %collective-permute-start.2 = (bf16[256,2,128]{2,0,1:T(8,128)(2,1)}, bf16[256,2,128]{2,0,1:T(8,128)(2,1)S(1)}, u32[]{:S(2)}, u32[]{:S(2)}) collective-permute-start(bf16[256,2,128]{2,0,1:T(8,128)(2,1)} %get-tuple-element.384), channel_id=1, source_target_pairs={{0,4},{4,8},{8,12},{12,16},{16,20},{20,24},{24,28},{1,5},{5,9},{9,... | collective-permute-start | bytes 393224 | tf_op jit(solution)/shard_map/while/body/eval_jaxpr/ppermute | solution.py:18
  47.6 11.2 %collective-permute-start = (s32[256]{0:T(256)S(1)}, s32[256]{0:T(256)S(1)}, u32[]{:S(2)}, u32[]{:S(2)}) collective-permute-start(s32[256]{0:T(256)S(1)} %get-tuple-element.385), channel_id=1, source_target_pairs={{0,4},{4,8},{8,12},{12,16},{16,20},{20,24},{24,28},{1,5},{5,9},{9,... | collective-permute-start | bytes 3080 | tf_op jit(solution)/shard_map/while/body/eval_jaxpr/ppermute | solution.py:18
  51.8 7.6 %collective-permute-start.1 = (bf16[256,2,128]{2,0,1:T(8,128)(2,1)}, bf16[256,2,128]{2,0,1:T(8,128)(2,1)S(1)}, u32[]{:S(2)}, u32[]{:S(2)}) collective-permute-start(bf16[256,2,128]{2,0,1:T(8,128)(2,1)} %get-tuple-element.383), channel_id=1, source_target_pairs={{0,4},{4,8},{8,12},{12,16},{16,20},{20,24},{24,28},{1,5},{5,9},{9,... | collective-permute-start | bytes 393224 | tf_op jit(solution)/shard_map/while/body/eval_jaxpr/ppermute | solution.py:18
  56.6 5.3 %collective-permute-start.2 = (bf16[256,2,128]{2,0,1:T(8,128)(2,1)}, bf16[256,2,128]{2,0,1:T(8,128)(2,1)S(1)}, u32[]{:S(2)}, u32[]{:S(2)}) collective-permute-start(bf16[256,2,128]{2,0,1:T(8,128)(2,1)} %get-tuple-element.384), channel_id=1, source_target_pairs={{0,4},{4,8},{8,12},{12,16},{16,20},{20,24},{24,28},{1,5},{5,9},{9,... | collective-permute-start | bytes 393224 | tf_op jit(solution)/shard_map/while/body/eval_jaxpr/ppermute | solution.py:18
  64.4 11.4 %collective-permute-start = (s32[256]{0:T(256)S(1)}, s32[256]{0:T(256)S(1)}, u32[]{:S(2)}, u32[]{:S(2)}) collective-permute-start(s32[256]{0:T(256)S(1)} %get-tuple-element.385), channel_id=1, source_target_pairs={{0,4},{4,8},{8,12},{12,16},{16,20},{20,24},{24,28},{1,5},{5,9},{9,... | collective-permute-start | bytes 3080 | tf_op jit(solution)/shard_map/while/body/eval_jaxpr/ppermute | solution.py:18
  68.7 8.0 %collective-permute-start.1 = (bf16[256,2,128]{2,0,1:T(8,128)(2,1)}, bf16[256,2,128]{2,0,1:T(8,128)(2,1)S(1)}, u32[]{:S(2)}, u32[]{:S(2)}) collective-permute-start(bf16[256,2,128]{2,0,1:T(8,128)(2,1)} %get-tuple-element.383), channel_id=1, source_target_pairs={{0,4},{4,8},{8,12},{12,16},{16,20},{20,24},{24,28},{1,5},{5,9},{9,... | collective-permute-start | bytes 393224 | tf_op jit(solution)/shard_map/while/body/eval_jaxpr/ppermute | solution.py:18
  73.9 5.3 %collective-permute-start.2 = (bf16[256,2,128]{2,0,1:T(8,128)(2,1)}, bf16[256,2,128]{2,0,1:T(8,128)(2,1)S(1)}, u32[]{:S(2)}, u32[]{:S(2)}) collective-permute-start(bf16[256,2,128]{2,0,1:T(8,128)(2,1)} %get-tuple-element.384), channel_id=1, source_target_pairs={{0,4},{4,8},{8,12},{12,16},{16,20},{20,24},{24,28},{1,5},{5,9},{9,... | collective-permute-start | bytes 393224 | tf_op jit(solution)/shard_map/while/body/eval_jaxpr/ppermute | solution.py:18
  81.8 10.0 %collective-permute-start = (s32[256]{0:T(256)S(1)}, s32[256]{0:T(256)S(1)}, u32[]{:S(2)}, u32[]{:S(2)}) collective-permute-start(s32[256]{0:T(256)S(1)} %get-tuple-element.385), channel_id=1, source_target_pairs={{0,4},{4,8},{8,12},{12,16},{16,20},{20,24},{24,28},{1,5},{5,9},{9,... | collective-permute-start | bytes 3080 | tf_op jit(solution)/shard_map/while/body/eval_jaxpr/ppermute | solution.py:18
  86.0 6.6 %collective-permute-start.1 = (bf16[256,2,128]{2,0,1:T(8,128)(2,1)}, bf16[256,2,128]{2,0,1:T(8,128)(2,1)S(1)}, u32[]{:S(2)}, u32[]{:S(2)}) collective-permute-start(bf16[256,2,128]{2,0,1:T(8,128)(2,1)} %get-tuple-element.383), channel_id=1, source_target_pairs={{0,4},{4,8},{8,12},{12,16},{16,20},{20,24},{24,28},{1,5},{5,9},{9,... | collective-permute-start | bytes 393224 | tf_op jit(solution)/shard_map/while/body/eval_jaxpr/ppermute | solution.py:18
  89.8 5.3 %collective-permute-start.2 = (bf16[256,2,128]{2,0,1:T(8,128)(2,1)}, bf16[256,2,128]{2,0,1:T(8,128)(2,1)S(1)}, u32[]{:S(2)}, u32[]{:S(2)}) collective-permute-start(bf16[256,2,128]{2,0,1:T(8,128)(2,1)} %get-tuple-element.384), channel_id=1, source_target_pairs={{0,4},{4,8},{8,12},{12,16},{16,20},{20,24},{24,28},{1,5},{5,9},{9,... | collective-permute-start | bytes 393224 | tf_op jit(solution)/shard_map/while/body/eval_jaxpr/ppermute | solution.py:18
